TPU v7x, 256 devices: a whole 4x4x8 slice. The times are simulated.
256 devices in a mesh: tm: 16 (over z, core), space: 16 (over y, x).
Axes of the slice: x: 4, y: 4, z: 8, core: 2. Of those that a mesh axis runs over, the one named last changes fastest.
Arguments:
- initial: float32 [2, 512, 512], P(None, 'space'), may hold values from 0.2 to 1
- guess: float32 [256, 2, 512, 512], P('tm', None, 'space'), may hold values from 0 to 1
- kappa: float32 [2, 512, 512], P(None, 'space'), may hold values from 0.005 to 0.05
- feed: float32 [512, 512], P('space'), may hold values from 0.002 to 0.01
- kill: float32 [512, 512], P('space'), may hold values from 0.002 to 0.008
- react: float32 [512, 512], P('space'), may hold values from 0.002 to 0.008
Outputs:
- solution: float32 [256, 2, 512, 512], P('tm', None, 'space')
All inputs are finite; a program needn't handle non-finite values.
Results may differ from a plain program's by a relative error of at most 0.00002.
Values sent between devices are 32-bit elements; how exact they have to be, the bound alone decides.
No kernel may reach another device: no remote copies, remote signals or barrier semaphores. Data moves between devices by JAX's collectives and lax.ppermute only.
A program may use at most 128 MiB of HBM per device.

v0:
```python
import jax
import jax.numpy as jnp
from jax import lax
from jax.sharding import Mesh
from jax.sharding import PartitionSpec as P

SPAN = 8
SPACE = ("space_0", "space_1")
TM = ("tm_0", "tm_1")
TM_SPACE = ("tm_0", "tm_1", "space_0", "space_1")


def padded_2(block, sides, width):
    for axis, dim in sides:
        count = lax.axis_size(axis)
        forward = [(i, i + 1) for i in range(count - 1)]
        backward = [(target, source) for source, target in forward]
        low = lax.ppermute(
            lax.slice_in_dim(block, block.shape[dim] - width, None, axis=dim), axis, forward
        )
        high = lax.ppermute(lax.slice_in_dim(block, 0, width, axis=dim), axis, backward)
        block = jnp.concatenate([low, block, high], axis=dim)
    return block


def shifted(block, axis, distance):
    devices = range(lax.axis_size(axis))
    route = [(i - distance, i) for i in devices if i - distance in devices]
    return lax.ppermute(block, axis, route)


def in_order(parts, dim):
    shape = list(parts.shape[1:])
    shape[dim] *= parts.shape[0]
    return jnp.moveaxis(parts, 0, dim).reshape(shape)


def gather_in_order(x, axes, turns):
    parts = x[None]
    for k in turns:
        parts = lax.all_gather(parts, axes[k], axis=0, tiled=True)
    carried = [lax.axis_size(axes[k]) for k in reversed(turns)]
    parts = parts.reshape(*carried, *x.shape)
    turned = sorted(range(len(turns)), key=lambda place: turns[len(turns) - 1 - place])
    return parts.transpose(*turned, *range(len(turns), parts.ndim)).reshape(-1, *x.shape)


def gather_axes(x, axes, turns, dim):
    return in_order(gather_in_order(x, axes, turns), dim)


def coarsen(field):
    shape = field.shape
    blocks = field.reshape(shape[:-2] + (shape[-2] // 2, 2, shape[-1] // 2, 2))
    return blocks.mean(axis=(-3, -1))


def refine(field):
    return jnp.repeat(jnp.repeat(field, 2, axis=-2), 2, axis=-1)


def advance(state, row_padded, coeffs):
    spread, supply, removal, coupling = coeffs
    padded = jnp.pad(row_padded, [(0, 0)] * (row_padded.ndim - 1) + [(1, 1)])
    laplace = (
        padded[..., :-2, 1:-1]
        + padded[..., 2:, 1:-1]
        + padded[..., 1:-1, :-2]
        + padded[..., 1:-1, 2:]
        - 4.0 * state
    )
    first_species = state[..., 0, :, :]
    second_species = state[..., 1, :, :]
    coupled = coupling * first_species * second_species * second_species
    next_first = (
        first_species + spread[0] * laplace[..., 0, :, :] - coupled + supply * (1.0 - first_species)
    )
    next_second = (
        second_species
        + spread[1] * laplace[..., 1, :, :]
        + coupled
        - (supply + removal) * second_species
    )
    return jnp.stack([next_first, next_second], axis=-3)


def margin_advance(state, coeffs, inside_mask):
    row_padded = jnp.pad(state, [(0, 0)] * (state.ndim - 2) + [(1, 1), (0, 0)])
    return advance(state, row_padded, coeffs) * inside_mask


def inside_rows(strip_rows, margin):
    global_rows = (
        lax.axis_index(SPACE) * strip_rows
        - margin
        + jnp.arange(strip_rows + 2 * margin, dtype=jnp.int32)
    )
    inside_mask = (global_rows >= 0) & (global_rows < strip_rows * lax.axis_size(SPACE))
    return inside_mask.astype(jnp.float32)[:, None]


def split_coeffs(packed):
    return (packed[0:2], packed[2], packed[3], packed[4])


def pack_coeffs(coeffs):
    return jnp.concatenate([coeffs[0], coeffs[1][None], coeffs[2][None], coeffs[3][None]])


def local(initial, guess, kappa, feed, kill, react):
    group = SPAN // 2
    time_index = lax.axis_index(TM)
    opening = time_index == 0
    member = time_index % group
    holder = member == group - 1
    level_zero = (kappa, feed, kill, react)
    spread_one = coarsen(kappa)
    supply_one = coarsen(feed)
    removal_one = coarsen(kill)
    coupling_one = coarsen(react)
    level_one = (2.0 * spread_one, 8.0 * supply_one, 8.0 * removal_one, 8.0 * coupling_one)
    level_two = (
        4.0 * coarsen(spread_one),
        64.0 * coarsen(supply_one),
        64.0 * coarsen(removal_one),
        64.0 * coarsen(coupling_one),
    )
    start_one = coarsen(initial)
    start_two = coarsen(start_one)
    strip_rows = initial.shape[-2]
    mid_rows = strip_rows // 2
    margin = SPAN - 1

    def fine_step(state):
        row_padded = padded_2(state, ((SPACE, 2),), 1)
        return advance(state, row_padded, level_zero)

    def fine_relax(series):
        incoming = shifted(series[-1], TM, 1)
        incoming = jnp.where(opening, initial, incoming)
        current = jnp.stack([incoming, series[SPAN - 1]])
        early = []
        later = []
        widened = padded_2(current, ((SPACE, 2),), margin)
        for position in range(SPAN - 1):
            widened = margin_advance(widened, fine_wide_coeffs, fine_mask)
            early.append(widened[0, :, margin : margin + strip_rows])
            later.append(widened[1, :, margin : margin + strip_rows])
        return (jnp.stack(early + [series[SPAN - 1]] + later + [series[-1]]), incoming)

    def mid_relax(values):
        predicted = values[1]
        for section in range(group):
            incoming = shifted(values[1], TM, 1)
            incoming = jnp.where(opening, start_one, incoming)
            widened = padded_2(incoming, ((SPACE, 1),), 2)
            first_wide = margin_advance(widened, mid_wide_coeffs, mid_mask) + mid_wide_forcing[0]
            second_wide = (
                margin_advance(first_wide, mid_wide_coeffs, mid_mask) + mid_wide_forcing[1]
            )
            fresh_first = first_wide[:, 2 : 2 + mid_rows]
            predicted = second_wide[:, 2 : 2 + mid_rows]
            fresh_second = predicted if section < group - 1 else values[1]
            values = jnp.where(member == section, jnp.stack([fresh_first, fresh_second]), values)
        return (values, predicted)

    fine_wide = padded_2(pack_coeffs(level_zero), ((SPACE, 1),), margin)
    fine_wide_coeffs = split_coeffs(fine_wide)
    fine_mask = inside_rows(strip_rows, margin)
    mid_mask = inside_rows(mid_rows, 2)
    series, incoming = fine_relax(guess)
    updated = fine_step(jnp.stack([series[SPAN - 2], series[-2]]))
    series = series.at[SPAN - 1].set(updated[0]).at[-1].set(updated[1])
    series, incoming = fine_relax(series)
    ends = jnp.stack([series[SPAN - 1], series[-1]])
    residual = fine_step(jnp.stack([series[SPAN - 2], series[-2]])) - ends
    restricted = coarsen(ends)
    earlier = jnp.stack([coarsen(incoming), restricted[0]])
    row_padded = padded_2(earlier, ((SPACE, 2),), 1)
    forcing_one = coarsen(residual) + restricted - advance(earlier, row_padded, level_one)
    mid_packed = jnp.concatenate(
        [pack_coeffs(level_one), forcing_one.reshape((4,) + forcing_one.shape[-2:])]
    )
    mid_wide = padded_2(mid_packed, ((SPACE, 1),), 2)
    mid_wide_coeffs = split_coeffs(mid_wide)
    mid_wide_forcing = mid_wide[5:9].reshape((2, 2) + mid_wide.shape[-2:])
    middle, predicted = mid_relax(restricted)
    coarse_values = coarsen(middle[1])
    coarse_right = coarsen(predicted - middle[1]) + coarse_values
    tm_count = lax.axis_size(TM)
    space_count = lax.axis_size(SPACE)
    rows_two = coarse_values.shape[-2]
    cols_two = coarse_values.shape[-1]
    quarter = cols_two // group
    reach = tm_count // group
    stacked = jnp.concatenate([coarse_values, coarse_right])
    held_piece = stacked[..., (group - 1) * quarter :]
    for distance in range(1, group):
        sent_part = stacked[..., (group - 1 - distance) * quarter : (group - distance) * quarter]
        arriving = shifted(sent_part, TM, -distance)
        held_piece = jnp.where(member == group - 1 - distance, arriving, held_piece)
    gathered = gather_axes(held_piece[None], TM_SPACE, (0, 2, 3, 1), 0)
    arranged = gathered.reshape((tm_count // group, group, space_count, 4, rows_two, quarter))
    arranged = jnp.transpose(arranged, (0, 3, 2, 4, 1, 5)).reshape(
        (tm_count // group, 4, space_count * rows_two, cols_two)
    )
    padded_held = jnp.pad(arranged, ((0, 0), (0, 0), (reach, reach), (0, 0)))
    window = lax.dynamic_slice_in_dim(
        padded_held, lax.axis_index(SPACE) * rows_two, rows_two + 2 * reach, 2
    )
    held_values = window[:, 0:2]
    held_right = window[:, 2:4]
    packed = jnp.concatenate([pack_coeffs(level_two), start_two])
    widened = padded_2(packed, ((SPACE, 1),), reach)
    wide_coeffs = split_coeffs(widened)
    wide_start = widened[5:7]
    coarse_mask = inside_rows(rows_two, reach)

    def wide_step(state):
        return margin_advance(state, wide_coeffs, coarse_mask)

    coarse_prev = jnp.concatenate([wide_start[None], held_values[:-1]])
    forcing_two = held_right - wide_step(coarse_prev)

    def march(previous, forcing_step):
        following = wide_step(previous) + forcing_step
        return (following, following)

    unused, solved = lax.scan(march, wide_start, forcing_two)
    own_point = time_index // group
    wide_change = lax.dynamic_index_in_dim(solved, own_point, 0, False) - lax.dynamic_index_in_dim(
        held_values, own_point, 0, False
    )
    correction = wide_change[:, reach : reach + rows_two]
    middle = middle.at[1].set(jnp.where(holder, middle[1] + refine(correction), middle[1]))
    middle, predicted = mid_relax(middle)
    change = refine(middle - restricted)
    series = series.at[SPAN - 1].add(change[0]).at[-1].add(change[1])
    series, incoming = fine_relax(series)
    return series


def solution(mesh):
    split = Mesh(mesh.devices.reshape(8, 2, 4, 4), ("tm_0", "tm_1", "space_0", "space_1"))
    placed = (
        P(None, SPACE, None),
        P(TM, None, SPACE, None),
        P(None, SPACE, None),
        P(SPACE, None),
        P(SPACE, None),
        P(SPACE, None),
    )
    return jax.shard_map(
        local, mesh=split, in_specs=placed, out_specs=P(TM, None, SPACE, None), check_vma=False
    )
```

profile of v0, /device:TPU:134, one launch (start us, length us, event | category | flops | bytes accessed | tf_op | source)
XLA Modules:
  0.0 520.0 jit_solution(8484025513956494548)
XLA Ops:
  17.1 6.4 %reshape.425 = f32[16,2,256,2]{3,2,1,0:T(8,128)} reshape(f32[32,512]{1,0:T(8,128)} %param.21) | data formatting | bytes 131072 | tf_op jit(solution)/shard_map/reshape | solution.py:54
  23.5 5.5 %reshape.426 = f32[16,2,256,2]{3,2,1,0:T(8,128)} reshape(f32[32,512]{1,0:T(8,128)S(1)} %copy-done.4) | data formatting | bytes 131072 | tf_op jit(solution)/shard_map/reshape | solution.py:54
  29.1 5.6 %reshape.427 = f32[16,2,256,2]{3,2,1,0:T(8,128)} reshape(f32[32,512]{1,0:T(8,128)S(1)} %copy-done.3) | data formatting | bytes 131072 | tf_op jit(solution)/shard_map/reshape | solution.py:54
  34.6 9.8 %reshape.424 = f32[2,16,2,256,2]{4,3,2,1,0:T(8,128)} reshape(f32[2,32,512]{2,1,0:T(8,128)S(1)} %copy-done.1) | data formatting | bytes 262144 | tf_op jit(solution)/shard_map/reshape | solution.py:54
  57.8 5.5 %collective-permute-start.1 = (f32[2,2,7,512]{3,1,2,0:T(2,128)S(1)}, f32[2,2,7,512]{3,1,2,0:T(2,128)S(1)}, u32[]{:S(2)}, u32[]{:S(2)}) collective-permute-start(f32[2,2,7,512]{3,1,2,0:T(2,128)S(1)} %copy.483), channel_id=1, source_target_pairs={{0,1},{1,2},{2,3},{3,4},{4,5},{5,6},{6,7},{7,8},{8,9},{9,10},{10,1... | collective-permute-start | bytes 172040 | tf_op jit(solution)/shard_map/ppermute | solution.py:18
  65.6 6.0 %collective-permute-done.2 = f32[2,2,7,512]{3,1,2,0:T(2,128)S(1)} collective-permute-done((f32[2,2,7,512]{3,1,2,0:T(2,128)S(1)}, f32[2,2,7,512]{3,1,2,0:T(2,128)S(1)}, u32[]{:S(2)}, u32[]{:S(2)}) %collective-permute-start.2) | collective-permute-done | bytes 57376 | tf_op jit(solution)/shard_map/ppermute | solution.py:21
  81.7 9.8 %reshape.422 = f32[2,16,2,256,2]{4,3,2,1,0:T(8,128)} reshape(f32[2,32,512]{2,1,0:T(8,128)S(1)} %copy-done.2) | data formatting | bytes 262144 | tf_op jit(solution)/shard_map/reshape | solution.py:54
  96.7 18.1 %reshape.423 = f32[2,2,16,2,256,2]{5,4,3,2,1,0:T(8,128)} reshape(f32[2,2,32,512]{3,2,1,0:T(8,128)S(1)} %pad_maximum_fusion.4) | data formatting | bytes 524288 | tf_op jit(solution)/shard_map/reshape | solution.py:54
  114.8 8.0 %reduce_sum.136 = f32[2,2,16,256]{3,2,1,0:T(8,128)S(1)} reduce(f32[2,2,16,2,256,2]{5,4,3,2,1,0:T(8,128)} %reshape.423, f32[]{:T(128)} %constant.259.clone.1), dimensions={3,5}, to_apply=%region_1.2 | reduce | flops 49152 | bytes 327684 | tf_op jit(solution)/shard_map/reduce_sum | solution.py:55
  135.8 9.8 %stack.349 = f32[1,2,16,2,256,2]{5,4,3,2,1,0:T(8,128)} reshape(f32[1,2,32,512]{3,2,1,0:T(8,128)S(1)} %get-tuple-element.295) | data formatting | bytes 262144 | tf_op jit(solution)/shard_map/stack | solution.py:175
  145.6 9.7 %stack.348 = f32[1,2,16,2,256,2]{5,4,3,2,1,0:T(8,128)} reshape(f32[1,2,32,512]{3,2,1,0:T(8,128)S(1)} %get-tuple-element.296) | data formatting | bytes 262144 | tf_op jit(solution)/shard_map/stack | solution.py:175
  155.3 5.2 %copy.505 = f32[1,2,16,2,256,2]{4,2,5,3,1,0:T(8,128)S(1)} copy(f32[1,2,16,2,256,2]{5,4,3,2,1,0:T(8,128)} %stack.348) | data formatting | bytes 262144 | tf_op jit(solution)/shard_map/stack | solution.py:175
  160.5 5.2 %copy.506 = f32[1,2,16,2,256,2]{4,2,5,3,1,0:T(8,128)S(1)} copy(f32[1,2,16,2,256,2]{5,4,3,2,1,0:T(8,128)} %stack.349) | data formatting | bytes 262144 | tf_op jit(solution)/shard_map/stack | solution.py:175
  165.8 9.8 %reshape.428 = f32[2,16,2,256,2]{4,3,2,1,0:T(8,128)} reshape(f32[2,32,512]{2,1,0:T(8,128)S(1)} %broadcast_select_fusion) | data formatting | bytes 262144 | tf_op jit(solution)/shard_map/reshape | solution.py:54
  180.2 6.0 %collective-permute-start.15 = (f32[2,2,1,256]{3,2,1,0:T(1,128)S(1)}, f32[2,2,1,256]{3,2,1,0:T(1,128)S(1)}, u32[]{:S(2)}, u32[]{:S(2)}) collective-permute-start(f32[2,2,1,256]{3,2,1,0:T(1,128)S(1)} %get-tuple-element.342), channel_id=1, source_target_pairs={{0,1},{1,2},{2,3},{3,4},{4,5},{5,6},{6,7},{7,8},{8,9},{9,10},{10,1... | collective-permute-start | bytes 12296 | tf_op jit(solution)/shard_map/ppermute | solution.py:18
  188.3 6.0 %collective-permute-start.11 = (f32[2,2,7,512]{3,1,2,0:T(2,128)S(1)}, f32[2,2,7,512]{3,1,2,0:T(2,128)S(1)}, u32[]{:S(2)}, u32[]{:S(2)}) collective-permute-start(f32[2,2,7,512]{3,1,2,0:T(2,128)S(1)} %copy.493), channel_id=1, source_target_pairs={{0,1},{1,2},{2,3},{3,4},{4,5},{5,6},{6,7},{7,8},{8,9},{9,10},{10,1... | collective-permute-start | bytes 172040 | tf_op jit(solution)/shard_map/ppermute | solution.py:18
  196.6 6.0 %collective-permute-done.12 = f32[2,2,7,512]{3,1,2,0:T(2,128)S(1)} collective-permute-done((f32[2,2,7,512]{3,1,2,0:T(2,128)S(1)}, f32[2,2,7,512]{3,1,2,0:T(2,128)S(1)}, u32[]{:S(2)}, u32[]{:S(2)}) %collective-permute-start.12) | collective-permute-done | bytes 57376 | tf_op jit(solution)/shard_map/ppermute | solution.py:21
  216.9 9.8 %stack.345 = f32[2,1,16,2,256,2]{5,4,3,2,0,1:T(8,128)} reshape(f32[2,1,32,512]{3,2,1,0:T(8,128)S(1)} %get-tuple-element.276) | data formatting | bytes 262144 | tf_op jit(solution)/shard_map/stack | solution.py:84
  226.7 5.2 %copy.503 = f32[2,1,16,2,256,2]{4,2,5,3,1,0:T(8,128)S(1)} copy(f32[2,1,16,2,256,2]{5,4,3,2,0,1:T(8,128)} %stack.345) | data formatting | bytes 262144 | tf_op jit(solution)/shard_map/stack | solution.py:84
  231.9 9.8 %stack.346 = f32[2,1,16,2,256,2]{5,4,3,2,0,1:T(8,128)} reshape(f32[2,1,32,512]{3,2,1,0:T(8,128)S(1)} %get-tuple-element.277) | data formatting | bytes 262144 | tf_op jit(solution)/shard_map/stack | solution.py:84
  329.6 25.1 %all-gather = f32[32,8,32]{2,1,0:T(8,128)S(1)} all-gather(f32[4,8,32]{2,1,0:T(8,128)S(1)} %fusion.421), channel_id=2, replica_groups=mesh['tm_0'=8,'tm_1'=2,'space_0'=4,'space_1'=4] {'tm_0'}, dimensions={0}, use_global_device_ids=true | all-gather | bytes 36864 | tf_op jit(solution)/shard_map/all_gather | solution.py:41
  354.7 13.0 %all_gather.13 = f32[32,1,4,8,32]{4,3,2,1,0:T(8,128)S(1)} all-gather(f32[8,1,4,8,32]{4,3,2,1,0:T(8,128)S(1)} %bitcast.180), channel_id=1, replica_groups=mesh['tm_0'=8,'tm_1'=2,'space_0'=4,'space_1'=4] {'space_0'}, dimensions={0}, use_global_device_ids=true | all-gather | bytes 163840 | tf_op jit(solution)/shard_map/all_gather | solution.py:41
  367.7 16.7 %all_gather.14 = f32[128,1,4,8,32]{4,3,2,1,0:T(8,128)} all-gather(f32[32,1,4,8,32]{4,3,2,1,0:T(8,128)S(1)} %all_gather.13), channel_id=1, replica_groups=mesh['tm_0'=8,'tm_1'=2,'space_0'=4,'space_1'=4] {'space_1'}, dimensions={0}, use_global_device_ids=true | all-gather | bytes 655360 | tf_op jit(solution)/shard_map/all_gather | solution.py:41
  402.3 5.4 %copy.511 = f32[256,1,4,8,32]{4,3,2,0,1:T(8,128)} copy(f32[256,1,4,8,32]{0,4,3,2,1:T(8,128)} %all-gather.3.cloned.1.call-done) | data formatting | bytes 2097152 | tf_op jit(solution)/shard_map/all_gather | solution.py:41
  (472 shorter events, 286.9 us)
Async XLA Ops:
  6.5 395.8 %all-gather.3.cloned.1.call-start = ((), (), s32[]{:S(2)}) async-start(), calls=%async_computation | async-start | bytes 1572864 | tf_op jit(solution)/shard_map/all_gather | solution.py:41
  7.5 50.2 %collective-permute-start = (f32[2,32,512]{2,1,0:T(8,128)S(1)}, f32[2,32,512]{2,1,0:T(8,128)S(1)}, u32[]{:S(2)}, u32[]{:S(2)}) collective-permute-start(f32[2,32,512]{2,1,0:T(8,128)S(1)} %get-tuple-element.232), channel_id=1, source_target_pairs={{0,16},{16,32},{32,48},{48,64},{64,80},{80,96},{96,112},{112,128},... | collective-permute-start | bytes 393224 | tf_op jit(solution)/shard_map/ppermute | solution.py:29
  10.3 47.2 %collective-permute-start.3 = (f32[5,7,512]{2,1,0:T(8,128)S(1)}, f32[5,7,512]{2,1,0:T(8,128)S(1)}, u32[]{:S(2)}, u32[]{:S(2)}) collective-permute-start(f32[5,7,512]{2,1,0:T(8,128)S(1)} %get-tuple-element.289), channel_id=1, source_target_pairs={{0,1},{1,2},{2,3},{3,4},{4,5},{5,6},{6,7},{7,8},{8,9},{9,10},{10,1... | collective-permute-start | bytes 215048 | tf_op jit(solution)/shard_map/ppermute | solution.py:18
  13.8 43.8 %collective-permute-start.4 = (f32[5,7,512]{2,1,0:T(8,128)S(1)}, f32[5,7,512]{2,1,0:T(8,128)S(1)}, u32[]{:S(2)}, u32[]{:S(2)}) collective-permute-start(f32[5,7,512]{2,1,0:T(8,128)S(1)} %get-tuple-element.290), channel_id=1, source_target_pairs={{1,0},{2,1},{3,2},{4,3},{5,4},{6,5},{7,6},{8,7},{9,8},{10,9},{11,1... | collective-permute-start | bytes 215048 | tf_op jit(solution)/shard_map/ppermute | solution.py:21
  57.8 7.8 %collective-permute-start.1 = (f32[2,2,7,512]{3,1,2,0:T(2,128)S(1)}, f32[2,2,7,512]{3,1,2,0:T(2,128)S(1)}, u32[]{:S(2)}, u32[]{:S(2)}) collective-permute-start(f32[2,2,7,512]{3,1,2,0:T(2,128)S(1)} %copy.483), channel_id=1, source_target_pairs={{0,1},{1,2},{2,3},{3,4},{4,5},{5,6},{6,7},{7,8},{8,9},{9,10},{10,1... | collective-permute-start | bytes 172040 | tf_op jit(solution)/shard_map/ppermute | solution.py:18
  63.4 8.2 %collective-permute-start.2 = (f32[2,2,7,512]{3,1,2,0:T(2,128)S(1)}, f32[2,2,7,512]{3,1,2,0:T(2,128)S(1)}, u32[]{:S(2)}, u32[]{:S(2)}) collective-permute-start(f32[2,2,7,512]{3,1,2,0:T(2,128)S(1)} %copy.484), channel_id=1, source_target_pairs={{1,0},{2,1},{3,2},{4,3},{5,4},{6,5},{7,6},{8,7},{9,8},{10,9},{11,1... | collective-permute-start | bytes 172040 | tf_op jit(solution)/shard_map/ppermute | solution.py:21
  75.8 20.3 %collective-permute-start.5 = (f32[2,2,1,512]{3,1,2,0:T(2,128)S(1)}, f32[2,2,1,512]{3,1,2,0:T(2,128)S(1)}, u32[]{:S(2)}, u32[]{:S(2)}) collective-permute-start(f32[2,2,1,512]{3,1,2,0:T(2,128)S(1)} %copy.487), channel_id=1, source_target_pairs={{0,1},{1,2},{2,3},{3,4},{4,5},{5,6},{6,7},{7,8},{8,9},{9,10},{10,1... | collective-permute-start | bytes 24584 | tf_op jit(solution)/shard_map/ppermute | solution.py:18
  77.7 18.4 %collective-permute-start.6 = (f32[2,2,1,512]{3,1,2,0:T(2,128)S(1)}, f32[2,2,1,512]{3,1,2,0:T(2,128)S(1)}, u32[]{:S(2)}, u32[]{:S(2)}) collective-permute-start(f32[2,2,1,512]{3,1,2,0:T(2,128)S(1)} %copy.489), channel_id=1, source_target_pairs={{1,0},{2,1},{3,2},{4,3},{5,4},{6,5},{7,6},{8,7},{9,8},{10,9},{11,1... | collective-permute-start | bytes 24584 | tf_op jit(solution)/shard_map/ppermute | solution.py:21
  124.8 41.0 %collective-permute-start.10 = (f32[2,32,512]{2,1,0:T(8,128)S(1)}, f32[2,32,512]{2,1,0:T(8,128)S(1)}, u32[]{:S(2)}, u32[]{:S(2)}) collective-permute-start(f32[2,32,512]{2,1,0:T(8,128)S(1)} %bitcast.176), channel_id=1, source_target_pairs={{0,16},{16,32},{32,48},{48,64},{64,80},{80,96},{96,112},{112,128},... | collective-permute-start | bytes 393224 | tf_op jit(solution)/shard_map/ppermute | solution.py:29
  129.3 36.4 %collective-permute-start.8 = (f32[2,2,256]{2,1,0:T(2,128)S(1)}, f32[2,2,256]{2,1,0:T(2,128)S(1)}, u32[]{:S(2)}, u32[]{:S(2)}) collective-permute-start(f32[2,2,256]{2,1,0:T(2,128)S(1)} %get-tuple-element.375), channel_id=1, source_target_pairs={{0,1},{1,2},{2,3},{3,4},{4,5},{5,6},{6,7},{7,8},{8,9},{9,10},{10,1... | collective-permute-start | bytes 12296 | tf_op jit(solution)/shard_map/ppermute | solution.py:18
  133.3 32.4 %collective-permute-start.9 = (f32[2,2,256]{2,1,0:T(2,128)S(1)}, f32[2,2,256]{2,1,0:T(2,128)S(1)}, u32[]{:S(2)}, u32[]{:S(2)}) collective-permute-start(f32[2,2,256]{2,1,0:T(2,128)S(1)} %get-tuple-element.376), channel_id=1, source_target_pairs={{1,0},{2,1},{3,2},{4,3},{5,4},{6,5},{7,6},{8,7},{9,8},{10,9},{11,1... | collective-permute-start | bytes 12296 | tf_op jit(solution)/shard_map/ppermute | solution.py:21
  180.2 16.1 %collective-permute-start.15 = (f32[2,2,1,256]{3,2,1,0:T(1,128)S(1)}, f32[2,2,1,256]{3,2,1,0:T(1,128)S(1)}, u32[]{:S(2)}, u32[]{:S(2)}) collective-permute-start(f32[2,2,1,256]{3,2,1,0:T(1,128)S(1)} %get-tuple-element.342), channel_id=1, source_target_pairs={{0,1},{1,2},{2,3},{3,4},{4,5},{5,6},{6,7},{7,8},{8,9},{9,10},{10,1... | collective-permute-start | bytes 12296 | tf_op jit(solution)/shard_map/ppermute | solution.py:18
  186.3 10.0 %collective-permute-start.16 = (f32[2,2,1,256]{3,2,1,0:T(1,128)S(1)}, f32[2,2,1,256]{3,2,1,0:T(1,128)S(1)}, u32[]{:S(2)}, u32[]{:S(2)}) collective-permute-start(f32[2,2,1,256]{3,2,1,0:T(1,128)S(1)} %get-tuple-element.343), channel_id=1, source_target_pairs={{1,0},{2,1},{3,2},{4,3},{5,4},{6,5},{7,6},{8,7},{9,8},{10,9},{11,1... | collective-permute-start | bytes 12296 | tf_op jit(solution)/shard_map/ppermute | solution.py:21
  188.3 8.3 %collective-permute-start.11 = (f32[2,2,7,512]{3,1,2,0:T(2,128)S(1)}, f32[2,2,7,512]{3,1,2,0:T(2,128)S(1)}, u32[]{:S(2)}, u32[]{:S(2)}) collective-permute-start(f32[2,2,7,512]{3,1,2,0:T(2,128)S(1)} %copy.493), channel_id=1, source_target_pairs={{0,1},{1,2},{2,3},{3,4},{4,5},{5,6},{6,7},{7,8},{8,9},{9,10},{10,1... | collective-permute-start | bytes 172040 | tf_op jit(solution)/shard_map/ppermute | solution.py:18
  194.4 8.2 %collective-permute-start.12 = (f32[2,2,7,512]{3,1,2,0:T(2,128)S(1)}, f32[2,2,7,512]{3,1,2,0:T(2,128)S(1)}, u32[]{:S(2)}, u32[]{:S(2)}) collective-permute-start(f32[2,2,7,512]{3,1,2,0:T(2,128)S(1)} %copy.494), channel_id=1, source_target_pairs={{1,0},{2,1},{3,2},{4,3},{5,4},{6,5},{7,6},{8,7},{9,8},{10,9},{11,1... | collective-permute-start | bytes 172040 | tf_op jit(solution)/shard_map/ppermute | solution.py:21
  208.7 7.7 %collective-permute-start.14 = (f32[2,2,1,512]{3,1,2,0:T(2,128)S(1)}, f32[2,2,1,512]{3,1,2,0:T(2,128)S(1)}, u32[]{:S(2)}, u32[]{:S(2)}) collective-permute-start(f32[2,2,1,512]{3,1,2,0:T(2,128)S(1)} %copy.499), channel_id=1, source_target_pairs={{1,0},{2,1},{3,2},{4,3},{5,4},{6,5},{7,6},{8,7},{9,8},{10,9},{11,1... | collective-permute-start | bytes 24584 | tf_op jit(solution)/shard_map/ppermute | solution.py:21
  249.0 7.8 %collective-permute-start.18 = (f32[9,2,256]{2,1,0:T(2,128)S(1)}, f32[9,2,256]{2,1,0:T(2,128)S(1)}, u32[]{:S(2)}, u32[]{:S(2)}) collective-permute-start(f32[9,2,256]{2,1,0:T(2,128)S(1)} %get-tuple-element.301), channel_id=1, source_target_pairs={{1,0},{2,1},{3,2},{4,3},{5,4},{6,5},{7,6},{8,7},{9,8},{10,9},{11,1... | collective-permute-start | bytes 55304 | tf_op jit(solution)/shard_map/ppermute | solution.py:21
  265.5 7.6 %collective-permute-start.21 = (f32[2,2,256]{2,1,0:T(2,128)S(1)}, f32[2,2,256]{2,1,0:T(2,128)S(1)}, u32[]{:S(2)}, u32[]{:S(2)}) collective-permute-start(f32[2,2,256]{2,1,0:T(2,128)S(1)} %get-tuple-element.372), channel_id=1, source_target_pairs={{1,0},{2,1},{3,2},{4,3},{5,4},{6,5},{7,6},{8,7},{9,8},{10,9},{11,1... | collective-permute-start | bytes 12296 | tf_op jit(solution)/shard_map/ppermute | solution.py:21
  318.3 11.1 %collective-permute-start.30 = (f32[4,8,32]{2,1,0:T(8,128)S(1)}, f32[4,8,32]{2,1,0:T(8,128)S(1)}, u32[]{:S(2)}, u32[]{:S(2)}) collective-permute-start(f32[4,8,32]{2,1,0:T(8,128)S(1)} %get-tuple-element.387), channel_id=1, source_target_pairs={{48,0},{64,16},{80,32},{96,48},{112,64},{128,80},{144,96},{160,112... | collective-permute-start | bytes 12296 | tf_op jit(solution)/shard_map/ppermute | solution.py:29
  320.3 9.2 %collective-permute-start.31 = (f32[4,8,32]{2,1,0:T(8,128)S(1)}, f32[4,8,32]{2,1,0:T(8,128)S(1)}, u32[]{:S(2)}, u32[]{:S(2)}) collective-permute-start(f32[4,8,32]{2,1,0:T(8,128)S(1)} %get-tuple-element.386), channel_id=1, source_target_pairs={{32,0},{48,16},{64,32},{80,48},{96,64},{112,80},{128,96},{144,112}... | collective-permute-start | bytes 12296 | tf_op jit(solution)/shard_map/ppermute | solution.py:29
  390.2 7.7 %collective-permute-start.29 = (f32[7,4,128]{2,1,0:T(4,128)S(1)}, f32[7,4,128]{2,1,0:T(4,128)S(1)}, u32[]{:S(2)}, u32[]{:S(2)}) collective-permute-start(f32[7,4,128]{2,1,0:T(4,128)S(1)} %get-tuple-element.378), channel_id=1, source_target_pairs={{1,0},{2,1},{3,2},{4,3},{5,4},{6,5},{7,6},{8,7},{9,8},{10,9},{11,1... | collective-permute-start | bytes 43016 | tf_op jit(solution)/shard_map/ppermute | solution.py:21
  430.4 7.6 %collective-permute-start.35 = (f32[2,2,256]{2,1,0:T(2,128)S(1)}, f32[2,2,256]{2,1,0:T(2,128)S(1)}, u32[]{:S(2)}, u32[]{:S(2)}) collective-permute-start(f32[2,2,256]{2,1,0:T(2,128)S(1)} %get-tuple-element.361), channel_id=1, source_target_pairs={{1,0},{2,1},{3,2},{4,3},{5,4},{6,5},{7,6},{8,7},{9,8},{10,9},{11,1... | collective-permute-start | bytes 12296 | tf_op jit(solution)/shard_map/ppermute | solution.py:21
  479.9 7.6 %collective-permute-start.44 = (f32[2,2,256]{2,1,0:T(2,128)S(1)}, f32[2,2,256]{2,1,0:T(2,128)S(1)}, u32[]{:S(2)}, u32[]{:S(2)}) collective-permute-start(f32[2,2,256]{2,1,0:T(2,128)S(1)} %get-tuple-element.355), channel_id=1, source_target_pairs={{1,0},{2,1},{3,2},{4,3},{5,4},{6,5},{7,6},{8,7},{9,8},{10,9},{11,1... | collective-permute-start | bytes 12296 | tf_op jit(solution)/shard_map/ppermute | solution.py:21
  498.0 8.2 %collective-permute-start.47 = (f32[2,2,7,512]{3,1,2,0:T(2,128)S(1)}, f32[2,2,7,512]{3,1,2,0:T(2,128)S(1)}, u32[]{:S(2)}, u32[]{:S(2)}) collective-permute-start(f32[2,2,7,512]{3,1,2,0:T(2,128)S(1)} %copy.524), channel_id=1, source_target_pairs={{1,0},{2,1},{3,2},{4,3},{5,4},{6,5},{7,6},{8,7},{9,8},{10,9},{11,1... | collective-permute-start | bytes 172040 | tf_op jit(solution)/shard_map/ppermute | solution.py:21
  (31 other events, 194.2 us)
Sparse Core Ops, SparseCore 0:
  388.0 14.2 all-gather.2
where the time goes:
time: 528 us; the launch traced here: 520 us
  local copies, waits for them, and re-layouts  169 us (32%)
  starting transfers between devices  135 us (26%)
  waiting for transfers between devices  87.7 us (17%)
  other arithmetic  56.9 us (11%)
  blocking collectives  54.8 us (10%)
  between operations  16.5 us (3%)
    reshape x8, local copies, waits for them, and re-layouts, coarsen(): blocks = field.reshape(shape[:-2] + (shape[-2] // 2, 2, shape[-1] // 2, 2))  68.5 us
    ppermute x17, starting transfers between devices, padded_2(): lax.ppermute(lax.slice_in_dim(block, 0, width, axis=dim), axis, backward)  56.9 us
    all_gather x3, blocking collectives, gather_in_order(): parts = lax.all_gather(parts, axes[k], axis=0, tiled=True)  54.8 us
    ppermute x17, waiting for transfers between devices, padded_2(): lax.ppermute(lax.slice_in_dim(block, 0, width, axis=dim), axis, backward)  51.3 us
    ppermute x17, starting transfers between devices, padded_2(): lax.ppermute(lax.slice_in_dim(block, block.shape[dim] - width, None, axis...  49.9 us
    reduce_sum x15, other arithmetic, coarsen(): return blocks.mean(axis=(-3, -1))  38.5 us
    ppermute x14, waiting for transfers between devices, shifted(): return lax.ppermute(block, axis, route)  32 us
    another operation x4, local copies, waits for them, and re-layouts, advance(): return jnp.stack([next_first, next_second], axis=-3)  30.1 us
  transfers between devices with their start and end apart: 49, of which 22 were waited for; matrix products, arithmetic and copies ran while one was open for 20% of the time, Pallas kernels for 0%

commit v1 on v0

--- a/solution.py
+++ b/solution.py
@@ -38,7 +38,9 @@
 def gather_in_order(x, axes, turns):
     parts = x[None]
     for k in turns:
-        parts = lax.all_gather(parts, axes[k], axis=0, tiled=True)
+        parts = jnp.concatenate(
+            lax.all_to_all(jnp.stack([parts] * lax.axis_size(axes[k])), axes[k], 0, 0), axis=0
+        )
     carried = [lax.axis_size(axes[k]) for k in reversed(turns)]
     parts = parts.reshape(*carried, *x.shape)
     turned = sorted(range(len(turns)), key=lambda place: turns[len(turns) - 1 - place])

time: 528 us -> 499 us (0.945)
  blocking collectives: 54.8 us -> 4.81 us
  starting transfers between devices: 135 us -> 154 us
  between operations: 16.5 us -> 3.12 us
  local copies, waits for them, and re-layouts: 169 us -> 176 us
    all_gather x3 -> x0, blocking collectives: 54.8 us -> none  [gather_in_order(): parts = lax.all_gather(parts, axes[k], axis=0, tiled=True)]
    all_to_all x0 -> x3, starting transfers between devices: none -> 18.8 us  [gather_in_order(): lax.all_to_all(jnp.stack([parts] * lax.axis_size(axes[k])), axes[k], 0, 0)]
    all_to_all x0 -> x3, waiting for transfers between devices: none -> 13 us  [gather_in_order(): lax.all_to_all(jnp.stack([parts] * lax.axis_size(axes[k])), axes[k], 0, 0)]
    all_gather x2 -> x0, local copies, waits for them, and re-layouts: 8.86 us -> none  [gather_in_order(): parts = lax.all_gather(parts, axes[k], axis=0, tiled=True)]
    unnamed x28 -> x36, local copies, waits for them, and re-layouts: 1.56 us -> 10 us
    ppermute x17, waiting for transfers between devices: 51.3 us -> 44.6 us  [padded_2(): lax.ppermute(lax.slice_in_dim(block, 0, width, axis=dim), axis, backward)]
  transfers between devices with their start and end apart: 49 -> 51, of which waited for: 22 -> 22; matrix products, arithmetic and copies ran while one was open for 20% -> 21% of each run, Pallas kernels for 0% -> 0%
where the time goes in v1:
time: 499 us; the launch traced here: 490 us
  local copies, waits for them, and re-layouts  176 us (35%)
  starting transfers between devices  154 us (31%)
  waiting for transfers between devices  91.4 us (18%)
  other arithmetic  60.9 us (12%)
    reshape x8, local copies, waits for them, and re-layouts, coarsen(): blocks = field.reshape(shape[:-2] + (shape[-2] // 2, 2, shape[-1] // 2, 2))  68.4 us
    ppermute x17, starting transfers between devices, padded_2(): lax.ppermute(lax.slice_in_dim(block, 0, width, axis=dim), axis, backward)  54.5 us
    ppermute x17, starting transfers between devices, padded_2(): lax.ppermute(lax.slice_in_dim(block, block.shape[dim] - width, None, axis...  52.3 us
    ppermute x17, waiting for transfers between devices, padded_2(): lax.ppermute(lax.slice_in_dim(block, 0, width, axis=dim), axis, backward)  44.6 us
    reduce_sum x15, other arithmetic, coarsen(): return blocks.mean(axis=(-3, -1))  38.5 us
    ppermute x14, waiting for transfers between devices, shifted(): return lax.ppermute(block, axis, route)  33.8 us
    another operation x4, local copies, waits for them, and re-layouts, advance(): return jnp.stack([next_first, next_second], axis=-3)  30 us
    another operation x4, local copies, waits for them, and re-layouts, local(): ends = jnp.stack([series[SPAN - 1], series[-1]])  29.9 us
  transfers between devices with their start and end apart: 51, of which 22 were waited for; matrix products, arithmetic and copies ran while one was open for 21% of the time, Pallas kernels for 0%

profile of v1, /device:TPU:134, one launch (start us, length us, event | category | flops | bytes accessed | tf_op | source)
XLA Modules:
  0.0 490.0 jit_solution(2194052150943166635)
XLA Ops:
  10.6 6.4 %reshape.432 = f32[16,2,256,2]{3,2,1,0:T(8,128)} reshape(f32[32,512]{1,0:T(8,128)} %param.21) | data formatting | bytes 131072 | tf_op jit(solution)/shard_map/reshape | solution.py:56
  17.0 5.5 %reshape.433 = f32[16,2,256,2]{3,2,1,0:T(8,128)} reshape(f32[32,512]{1,0:T(8,128)S(1)} %copy-done.4) | data formatting | bytes 131072 | tf_op jit(solution)/shard_map/reshape | solution.py:56
  22.5 5.6 %reshape.434 = f32[16,2,256,2]{3,2,1,0:T(8,128)} reshape(f32[32,512]{1,0:T(8,128)S(1)} %copy-done.3) | data formatting | bytes 131072 | tf_op jit(solution)/shard_map/reshape | solution.py:56
  28.1 9.8 %reshape.431 = f32[2,16,2,256,2]{4,3,2,1,0:T(8,128)} reshape(f32[2,32,512]{2,1,0:T(8,128)S(1)} %copy-done.1) | data formatting | bytes 262144 | tf_op jit(solution)/shard_map/reshape | solution.py:56
  51.2 5.5 %collective-permute-start.1 = (f32[2,2,7,512]{3,1,2,0:T(2,128)S(1)}, f32[2,2,7,512]{3,1,2,0:T(2,128)S(1)}, u32[]{:S(2)}, u32[]{:S(2)}) collective-permute-start(f32[2,2,7,512]{3,1,2,0:T(2,128)S(1)} %copy.483), channel_id=1, source_target_pairs={{0,1},{1,2},{2,3},{3,4},{4,5},{5,6},{6,7},{7,8},{8,9},{9,10},{10,1... | collective-permute-start | bytes 172040 | tf_op jit(solution)/shard_map/ppermute | solution.py:18
  59.0 6.0 %collective-permute-done.2 = f32[2,2,7,512]{3,1,2,0:T(2,128)S(1)} collective-permute-done((f32[2,2,7,512]{3,1,2,0:T(2,128)S(1)}, f32[2,2,7,512]{3,1,2,0:T(2,128)S(1)}, u32[]{:S(2)}, u32[]{:S(2)}) %collective-permute-start.2) | collective-permute-done | bytes 57376 | tf_op jit(solution)/shard_map/ppermute | solution.py:21
  75.1 9.8 %reshape.429 = f32[2,16,2,256,2]{4,3,2,1,0:T(8,128)} reshape(f32[2,32,512]{2,1,0:T(8,128)S(1)} %copy-done.2) | data formatting | bytes 262144 | tf_op jit(solution)/shard_map/reshape | solution.py:56
  90.0 18.1 %reshape.430 = f32[2,2,16,2,256,2]{5,4,3,2,1,0:T(8,128)} reshape(f32[2,2,32,512]{3,2,1,0:T(8,128)S(1)} %pad_maximum_fusion.5) | data formatting | bytes 524288 | tf_op jit(solution)/shard_map/reshape | solution.py:56
  108.1 8.0 %reduce_sum.136 = f32[2,2,16,256]{3,2,1,0:T(8,128)S(1)} reduce(f32[2,2,16,2,256,2]{5,4,3,2,1,0:T(8,128)} %reshape.430, f32[]{:T(128)} %constant.259.clone.1), dimensions={3,5}, to_apply=%region_1.2 | reduce | flops 49152 | bytes 327684 | tf_op jit(solution)/shard_map/reduce_sum | solution.py:57
  129.1 9.8 %stack.361 = f32[1,2,16,2,256,2]{5,4,3,2,1,0:T(8,128)} reshape(f32[1,2,32,512]{3,2,1,0:T(8,128)S(1)} %get-tuple-element.295) | data formatting | bytes 262144 | tf_op jit(solution)/shard_map/stack | solution.py:177
  138.9 9.7 %stack.360 = f32[1,2,16,2,256,2]{5,4,3,2,1,0:T(8,128)} reshape(f32[1,2,32,512]{3,2,1,0:T(8,128)S(1)} %get-tuple-element.296) | data formatting | bytes 262144 | tf_op jit(solution)/shard_map/stack | solution.py:177
  148.6 5.2 %copy.505 = f32[1,2,16,2,256,2]{4,2,5,3,1,0:T(8,128)S(1)} copy(f32[1,2,16,2,256,2]{5,4,3,2,1,0:T(8,128)} %stack.360) | data formatting | bytes 262144 | tf_op jit(solution)/shard_map/stack | solution.py:177
  153.8 5.2 %copy.506 = f32[1,2,16,2,256,2]{4,2,5,3,1,0:T(8,128)S(1)} copy(f32[1,2,16,2,256,2]{5,4,3,2,1,0:T(8,128)} %stack.361) | data formatting | bytes 262144 | tf_op jit(solution)/shard_map/stack | solution.py:177
  159.1 9.8 %reshape.435 = f32[2,16,2,256,2]{4,3,2,1,0:T(8,128)} reshape(f32[2,32,512]{2,1,0:T(8,128)S(1)} %broadcast_select_fusion) | data formatting | bytes 262144 | tf_op jit(solution)/shard_map/reshape | solution.py:56
  173.5 6.0 %collective-permute-start.15 = (f32[2,2,1,256]{3,2,1,0:T(1,128)S(1)}, f32[2,2,1,256]{3,2,1,0:T(1,128)S(1)}, u32[]{:S(2)}, u32[]{:S(2)}) collective-permute-start(f32[2,2,1,256]{3,2,1,0:T(1,128)S(1)} %get-tuple-element.342), channel_id=1, source_target_pairs={{0,1},{1,2},{2,3},{3,4},{4,5},{5,6},{6,7},{7,8},{8,9},{9,10},{10,1... | collective-permute-start | bytes 12296 | tf_op jit(solution)/shard_map/ppermute | solution.py:18
  181.5 6.0 %collective-permute-start.11 = (f32[2,2,7,512]{3,1,2,0:T(2,128)S(1)}, f32[2,2,7,512]{3,1,2,0:T(2,128)S(1)}, u32[]{:S(2)}, u32[]{:S(2)}) collective-permute-start(f32[2,2,7,512]{3,1,2,0:T(2,128)S(1)} %copy.493), channel_id=1, source_target_pairs={{0,1},{1,2},{2,3},{3,4},{4,5},{5,6},{6,7},{7,8},{8,9},{9,10},{10,1... | collective-permute-start | bytes 172040 | tf_op jit(solution)/shard_map/ppermute | solution.py:18
  189.8 6.0 %collective-permute-done.12 = f32[2,2,7,512]{3,1,2,0:T(2,128)S(1)} collective-permute-done((f32[2,2,7,512]{3,1,2,0:T(2,128)S(1)}, f32[2,2,7,512]{3,1,2,0:T(2,128)S(1)}, u32[]{:S(2)}, u32[]{:S(2)}) %collective-permute-start.12) | collective-permute-done | bytes 57376 | tf_op jit(solution)/shard_map/ppermute | solution.py:21
  210.1 9.8 %stack.357 = f32[2,1,16,2,256,2]{5,4,3,2,0,1:T(8,128)} reshape(f32[2,1,32,512]{3,2,1,0:T(8,128)S(1)} %get-tuple-element.276) | data formatting | bytes 262144 | tf_op jit(solution)/shard_map/stack | solution.py:86
  225.1 9.8 %stack.358 = f32[2,1,16,2,256,2]{5,4,3,2,0,1:T(8,128)} reshape(f32[2,1,32,512]{3,2,1,0:T(8,128)S(1)} %get-tuple-element.277) | data formatting | bytes 262144 | tf_op jit(solution)/shard_map/stack | solution.py:86
  321.9 7.9 %all-to-all-start = ((f32[8,1,1024]{2,1,0:T(1,128)}), f32[8,1,1024]{2,1,0:T(1,128)S(1)}, u32[]{:S(2)}, u32[]{:S(2)}) async-start(f32[8,1,1024]{2,1,0:T(1,128)} %reshape.443), calls=%async_computation | async-start | bytes 65536 | tf_op jit(solution)/shard_map/all_to_all | solution.py:42
  342.4 6.1 %all-to-all-done.1 = f32[4,1,8192]{2,1,0:T(1,128)S(1)} async-done(((f32[4,1,8192]{2,1,0:T(1,128)}), f32[4,1,8192]{2,1,0:T(1,128)S(1)}, u32[]{:S(2)}, u32[]{:S(2)}) %all-to-all-start.1) | async-done | bytes 131104 | tf_op jit(solution)/shard_map/all_to_all | solution.py:42
  354.2 6.7 %all-to-all-start.2 = ((f32[4,1,32768]{2,1,0:T(1,128)}), f32[4,1,32768]{2,1,0:T(1,128)S(1)}, u32[]{:S(2)}, u32[]{:S(2)}) async-start(f32[4,1,32768]{2,1,0:T(1,128)} %reshape.447), calls=%async_computation.2 | async-start | bytes 1048576 | tf_op jit(solution)/shard_map/all_to_all | solution.py:42
  360.8 6.9 %all-to-all-done.2 = f32[4,1,32768]{2,1,0:T(1,128)S(1)} async-done(((f32[4,1,32768]{2,1,0:T(1,128)}), f32[4,1,32768]{2,1,0:T(1,128)S(1)}, u32[]{:S(2)}, u32[]{:S(2)}) %all-to-all-start.2) | async-done | bytes 524320 | tf_op jit(solution)/shard_map/all_to_all | solution.py:42
  409.2 5.7 %collective-permute-done.35 = f32[2,2,256]{2,1,0:T(2,128)S(1)} collective-permute-done((f32[2,2,256]{2,1,0:T(2,128)S(1)}, f32[2,2,256]{2,1,0:T(2,128)S(1)}, u32[]{:S(2)}, u32[]{:S(2)}) %collective-permute-start.35) | collective-permute-done | bytes 4128 | tf_op jit(solution)/shard_map/ppermute | solution.py:21
  (487 shorter events, 302.7 us)
Async XLA Ops:
  1.0 50.1 %collective-permute-start = (f32[2,32,512]{2,1,0:T(8,128)S(1)}, f32[2,32,512]{2,1,0:T(8,128)S(1)}, u32[]{:S(2)}, u32[]{:S(2)}) collective-permute-start(f32[2,32,512]{2,1,0:T(8,128)S(1)} %get-tuple-element.232), channel_id=1, source_target_pairs={{0,16},{16,32},{32,48},{48,64},{64,80},{80,96},{96,112},{112,128},... | collective-permute-start | bytes 393224 | tf_op jit(solution)/shard_map/ppermute | solution.py:29
  3.8 47.2 %collective-permute-start.3 = (f32[5,7,512]{2,1,0:T(8,128)S(1)}, f32[5,7,512]{2,1,0:T(8,128)S(1)}, u32[]{:S(2)}, u32[]{:S(2)}) collective-permute-start(f32[5,7,512]{2,1,0:T(8,128)S(1)} %get-tuple-element.289), channel_id=1, source_target_pairs={{0,1},{1,2},{2,3},{3,4},{4,5},{5,6},{6,7},{7,8},{8,9},{9,10},{10,1... | collective-permute-start | bytes 215048 | tf_op jit(solution)/shard_map/ppermute | solution.py:18
  7.2 43.8 %collective-permute-start.4 = (f32[5,7,512]{2,1,0:T(8,128)S(1)}, f32[5,7,512]{2,1,0:T(8,128)S(1)}, u32[]{:S(2)}, u32[]{:S(2)}) collective-permute-start(f32[5,7,512]{2,1,0:T(8,128)S(1)} %get-tuple-element.290), channel_id=1, source_target_pairs={{1,0},{2,1},{3,2},{4,3},{5,4},{6,5},{7,6},{8,7},{9,8},{10,9},{11,1... | collective-permute-start | bytes 215048 | tf_op jit(solution)/shard_map/ppermute | solution.py:21
  51.2 7.8 %collective-permute-start.1 = (f32[2,2,7,512]{3,1,2,0:T(2,128)S(1)}, f32[2,2,7,512]{3,1,2,0:T(2,128)S(1)}, u32[]{:S(2)}, u32[]{:S(2)}) collective-permute-start(f32[2,2,7,512]{3,1,2,0:T(2,128)S(1)} %copy.483), channel_id=1, source_target_pairs={{0,1},{1,2},{2,3},{3,4},{4,5},{5,6},{6,7},{7,8},{8,9},{9,10},{10,1... | collective-permute-start | bytes 172040 | tf_op jit(solution)/shard_map/ppermute | solution.py:18
  56.8 8.2 %collective-permute-start.2 = (f32[2,2,7,512]{3,1,2,0:T(2,128)S(1)}, f32[2,2,7,512]{3,1,2,0:T(2,128)S(1)}, u32[]{:S(2)}, u32[]{:S(2)}) collective-permute-start(f32[2,2,7,512]{3,1,2,0:T(2,128)S(1)} %copy.484), channel_id=1, source_target_pairs={{1,0},{2,1},{3,2},{4,3},{5,4},{6,5},{7,6},{8,7},{9,8},{10,9},{11,1... | collective-permute-start | bytes 172040 | tf_op jit(solution)/shard_map/ppermute | solution.py:21
  69.2 20.3 %collective-permute-start.5 = (f32[2,2,1,512]{3,1,2,0:T(2,128)S(1)}, f32[2,2,1,512]{3,1,2,0:T(2,128)S(1)}, u32[]{:S(2)}, u32[]{:S(2)}) collective-permute-start(f32[2,2,1,512]{3,1,2,0:T(2,128)S(1)} %copy.487), channel_id=1, source_target_pairs={{0,1},{1,2},{2,3},{3,4},{4,5},{5,6},{6,7},{7,8},{8,9},{9,10},{10,1... | collective-permute-start | bytes 24584 | tf_op jit(solution)/shard_map/ppermute | solution.py:18
  71.1 18.4 %collective-permute-start.6 = (f32[2,2,1,512]{3,1,2,0:T(2,128)S(1)}, f32[2,2,1,512]{3,1,2,0:T(2,128)S(1)}, u32[]{:S(2)}, u32[]{:S(2)}) collective-permute-start(f32[2,2,1,512]{3,1,2,0:T(2,128)S(1)} %copy.489), channel_id=1, source_target_pairs={{1,0},{2,1},{3,2},{4,3},{5,4},{6,5},{7,6},{8,7},{9,8},{10,9},{11,1... | collective-permute-start | bytes 24584 | tf_op jit(solution)/shard_map/ppermute | solution.py:21
  118.1 41.0 %collective-permute-start.10 = (f32[2,32,512]{2,1,0:T(8,128)S(1)}, f32[2,32,512]{2,1,0:T(8,128)S(1)}, u32[]{:S(2)}, u32[]{:S(2)}) collective-permute-start(f32[2,32,512]{2,1,0:T(8,128)S(1)} %bitcast.184), channel_id=1, source_target_pairs={{0,16},{16,32},{32,48},{48,64},{64,80},{80,96},{96,112},{112,128},... | collective-permute-start | bytes 393224 | tf_op jit(solution)/shard_map/ppermute | solution.py:29
  122.6 36.4 %collective-permute-start.8 = (f32[2,2,256]{2,1,0:T(2,128)S(1)}, f32[2,2,256]{2,1,0:T(2,128)S(1)}, u32[]{:S(2)}, u32[]{:S(2)}) collective-permute-start(f32[2,2,256]{2,1,0:T(2,128)S(1)} %get-tuple-element.375), channel_id=1, source_target_pairs={{0,1},{1,2},{2,3},{3,4},{4,5},{5,6},{6,7},{7,8},{8,9},{9,10},{10,1... | collective-permute-start | bytes 12296 | tf_op jit(solution)/shard_map/ppermute | solution.py:18
  126.7 32.4 %collective-permute-start.9 = (f32[2,2,256]{2,1,0:T(2,128)S(1)}, f32[2,2,256]{2,1,0:T(2,128)S(1)}, u32[]{:S(2)}, u32[]{:S(2)}) collective-permute-start(f32[2,2,256]{2,1,0:T(2,128)S(1)} %get-tuple-element.376), channel_id=1, source_target_pairs={{1,0},{2,1},{3,2},{4,3},{5,4},{6,5},{7,6},{8,7},{9,8},{10,9},{11,1... | collective-permute-start | bytes 12296 | tf_op jit(solution)/shard_map/ppermute | solution.py:21
  173.5 16.1 %collective-permute-start.15 = (f32[2,2,1,256]{3,2,1,0:T(1,128)S(1)}, f32[2,2,1,256]{3,2,1,0:T(1,128)S(1)}, u32[]{:S(2)}, u32[]{:S(2)}) collective-permute-start(f32[2,2,1,256]{3,2,1,0:T(1,128)S(1)} %get-tuple-element.342), channel_id=1, source_target_pairs={{0,1},{1,2},{2,3},{3,4},{4,5},{5,6},{6,7},{7,8},{8,9},{9,10},{10,1... | collective-permute-start | bytes 12296 | tf_op jit(solution)/shard_map/ppermute | solution.py:18
  179.5 10.0 %collective-permute-start.16 = (f32[2,2,1,256]{3,2,1,0:T(1,128)S(1)}, f32[2,2,1,256]{3,2,1,0:T(1,128)S(1)}, u32[]{:S(2)}, u32[]{:S(2)}) collective-permute-start(f32[2,2,1,256]{3,2,1,0:T(1,128)S(1)} %get-tuple-element.343), channel_id=1, source_target_pairs={{1,0},{2,1},{3,2},{4,3},{5,4},{6,5},{7,6},{8,7},{9,8},{10,9},{11,1... | collective-permute-start | bytes 12296 | tf_op jit(solution)/shard_map/ppermute | solution.py:21
  181.5 8.3 %collective-permute-start.11 = (f32[2,2,7,512]{3,1,2,0:T(2,128)S(1)}, f32[2,2,7,512]{3,1,2,0:T(2,128)S(1)}, u32[]{:S(2)}, u32[]{:S(2)}) collective-permute-start(f32[2,2,7,512]{3,1,2,0:T(2,128)S(1)} %copy.493), channel_id=1, source_target_pairs={{0,1},{1,2},{2,3},{3,4},{4,5},{5,6},{6,7},{7,8},{8,9},{9,10},{10,1... | collective-permute-start | bytes 172040 | tf_op jit(solution)/shard_map/ppermute | solution.py:18
  187.6 8.2 %collective-permute-start.12 = (f32[2,2,7,512]{3,1,2,0:T(2,128)S(1)}, f32[2,2,7,512]{3,1,2,0:T(2,128)S(1)}, u32[]{:S(2)}, u32[]{:S(2)}) collective-permute-start(f32[2,2,7,512]{3,1,2,0:T(2,128)S(1)} %copy.494), channel_id=1, source_target_pairs={{1,0},{2,1},{3,2},{4,3},{5,4},{6,5},{7,6},{8,7},{9,8},{10,9},{11,1... | collective-permute-start | bytes 172040 | tf_op jit(solution)/shard_map/ppermute | solution.py:21
  201.9 7.7 %collective-permute-start.14 = (f32[2,2,1,512]{3,1,2,0:T(2,128)S(1)}, f32[2,2,1,512]{3,1,2,0:T(2,128)S(1)}, u32[]{:S(2)}, u32[]{:S(2)}) collective-permute-start(f32[2,2,1,512]{3,1,2,0:T(2,128)S(1)} %copy.499), channel_id=1, source_target_pairs={{1,0},{2,1},{3,2},{4,3},{5,4},{6,5},{7,6},{8,7},{9,8},{10,9},{11,1... | collective-permute-start | bytes 24584 | tf_op jit(solution)/shard_map/ppermute | solution.py:21
  242.2 7.8 %collective-permute-start.18 = (f32[9,2,256]{2,1,0:T(2,128)S(1)}, f32[9,2,256]{2,1,0:T(2,128)S(1)}, u32[]{:S(2)}, u32[]{:S(2)}) collective-permute-start(f32[9,2,256]{2,1,0:T(2,128)S(1)} %get-tuple-element.301), channel_id=1, source_target_pairs={{1,0},{2,1},{3,2},{4,3},{5,4},{6,5},{7,6},{8,7},{9,8},{10,9},{11,1... | collective-permute-start | bytes 55304 | tf_op jit(solution)/shard_map/ppermute | solution.py:21
  290.7 11.5 %collective-permute-start.26 = (f32[2,2,256]{2,1,0:T(2,128)S(1)}, f32[2,2,256]{2,1,0:T(2,128)S(1)}, u32[]{:S(2)}, u32[]{:S(2)}) collective-permute-start(f32[2,2,256]{2,1,0:T(2,128)S(1)} %get-tuple-element.367), channel_id=1, source_target_pairs={{0,1},{1,2},{2,3},{3,4},{4,5},{5,6},{6,7},{7,8},{8,9},{9,10},{10,1... | collective-permute-start | bytes 12296 | tf_op jit(solution)/shard_map/ppermute | solution.py:18
  292.6 9.6 %collective-permute-start.27 = (f32[2,2,256]{2,1,0:T(2,128)S(1)}, f32[2,2,256]{2,1,0:T(2,128)S(1)}, u32[]{:S(2)}, u32[]{:S(2)}) collective-permute-start(f32[2,2,256]{2,1,0:T(2,128)S(1)} %get-tuple-element.368), channel_id=1, source_target_pairs={{1,0},{2,1},{3,2},{4,3},{5,4},{6,5},{7,6},{8,7},{9,8},{10,9},{11,1... | collective-permute-start | bytes 12296 | tf_op jit(solution)/shard_map/ppermute | solution.py:21
  321.9 13.9 %all-to-all-start = ((f32[8,1,1024]{2,1,0:T(1,128)}), f32[8,1,1024]{2,1,0:T(1,128)S(1)}, u32[]{:S(2)}, u32[]{:S(2)}) async-start(f32[8,1,1024]{2,1,0:T(1,128)} %reshape.443), calls=%async_computation | async-start | bytes 65536 | tf_op jit(solution)/shard_map/all_to_all | solution.py:42
  329.8 12.6 %collective-permute-start.28 = (f32[7,4,128]{2,1,0:T(4,128)S(1)}, f32[7,4,128]{2,1,0:T(4,128)S(1)}, u32[]{:S(2)}, u32[]{:S(2)}) collective-permute-start(f32[7,4,128]{2,1,0:T(4,128)S(1)} %get-tuple-element.377), channel_id=1, source_target_pairs={{0,1},{1,2},{2,3},{3,4},{4,5},{5,6},{6,7},{7,8},{8,9},{9,10},{10,1... | collective-permute-start | bytes 43016 | tf_op jit(solution)/shard_map/ppermute | solution.py:18
  333.9 8.5 %collective-permute-start.29 = (f32[7,4,128]{2,1,0:T(4,128)S(1)}, f32[7,4,128]{2,1,0:T(4,128)S(1)}, u32[]{:S(2)}, u32[]{:S(2)}) collective-permute-start(f32[7,4,128]{2,1,0:T(4,128)S(1)} %get-tuple-element.378), channel_id=1, source_target_pairs={{1,0},{2,1},{3,2},{4,3},{5,4},{6,5},{7,6},{8,7},{9,8},{10,9},{11,1... | collective-permute-start | bytes 43016 | tf_op jit(solution)/shard_map/ppermute | solution.py:21
  338.2 10.3 %all-to-all-start.1 = ((f32[4,1,8192]{2,1,0:T(1,128)}), f32[4,1,8192]{2,1,0:T(1,128)S(1)}, u32[]{:S(2)}, u32[]{:S(2)}) async-start(f32[4,1,8192]{2,1,0:T(1,128)} %reshape.445), calls=%async_computation.1 | async-start | bytes 262144 | tf_op jit(solution)/shard_map/all_to_all | solution.py:42
  354.2 13.6 %all-to-all-start.2 = ((f32[4,1,32768]{2,1,0:T(1,128)}), f32[4,1,32768]{2,1,0:T(1,128)S(1)}, u32[]{:S(2)}, u32[]{:S(2)}) async-start(f32[4,1,32768]{2,1,0:T(1,128)} %reshape.447), calls=%async_computation.2 | async-start | bytes 1048576 | tf_op jit(solution)/shard_map/all_to_all | solution.py:42
  474.8 8.2 %collective-permute-start.47 = (f32[2,2,7,512]{3,1,2,0:T(2,128)S(1)}, f32[2,2,7,512]{3,1,2,0:T(2,128)S(1)}, u32[]{:S(2)}, u32[]{:S(2)}) collective-permute-start(f32[2,2,7,512]{3,1,2,0:T(2,128)S(1)} %copy.524), channel_id=1, source_target_pairs={{1,0},{2,1},{3,2},{4,3},{5,4},{6,5},{7,6},{8,7},{9,8},{10,9},{11,1... | collective-permute-start | bytes 172040 | tf_op jit(solution)/shard_map/ppermute | solution.py:21
  (33 other events, 205.2 us)
